TPU v7x, 256 devices: a whole 4x4x8 slice. The times are simulated.
256 devices in a mesh: ctx: 16 (over z_hi, x), tp: 4 (over y), dp: 4 (over z_lo, core).
Axes of the slice: x: 4, y: 4, z: 8 (z_hi: 4, z_lo: 2; z = z_hi * 2 + z_lo), core: 2. Of those that a mesh axis runs over, the one named last changes fastest.
Arguments:
- byte_embed: bfloat16 [65536, 1024], P(('dp', 'ctx', 'tp')), parts along dimension 0, may hold values from -6 to 6
- patch_start: int32 [65536], P(('dp', 'ctx', 'tp')), parts along dimension 0, may hold values from 0 to 1, as said below
- enc_gain: float32 [1024], replicated, may hold values from 0.1 to 1.9
- enc_qkv: bfloat16 [1024, 3072], replicated, may hold values from -4 to 4
- enc_out: bfloat16 [1024, 1024], replicated, may hold values from -0.1875 to 0.1875
- up_proj: bfloat16 [1024, 4096], P('ctx', 'tp'), may hold values from -0.1875 to 0.1875
- lat_gain: float32 [4096], replicated, may hold values from 0.1 to 1.9
- query_proj: bfloat16 [4096, 2048], P('ctx', 'tp'), may hold values from -4 to 4
- key_proj: bfloat16 [4096, 512], P('ctx', 'tp'), may hold values from -4 to 4
- value_matrix: bfloat16 [4096, 512], P('ctx', 'tp'), may hold values from -0.09375 to 0.09375
- out_proj: bfloat16 [2048, 4096], P('tp', 'ctx'), may hold values from -0.125 to 0.125
- down_proj: bfloat16 [4096, 1024], P('tp', 'ctx'), may hold values from -0.09375 to 0.09375
Outputs:
- byte_states: bfloat16 [65536, 1024], P(('dp', 'ctx', 'tp')), parts along dimension 0
There are 4 independent parts, one for each index of `dp`. A program takes and returns all parts, laid end to end along the dimension named above; an argument that names none is the same for every part. Nothing has to cross between parts.
Inputs may be any that keep to these rules, and one draw needn't show every extreme that they name: `patch_start`: byte 0 begins a patch; every patch spans 1 to 19 bytes; each aligned group of 1024 bytes holds at most 256 patch starts, and some group holds exactly 256.
All inputs are finite; a program needn't handle non-finite values.
Results may differ from a plain program's by a relative error of at most 0.015.
Values may be sent and summed in bfloat16 or wider, within the bound.
A program may use at most 128 MiB of HBM per device.

v0:
```python
import jax
import jax.numpy as jnp
from jax import lax
from jax.sharding import PartitionSpec as P

BH = 16
HB = 64
HEAD_SIZE = 128
WIN = 512
EPS = 1e-05


def shifted(block, axis, distance):
    devices = range(lax.axis_size(axis))
    route = [(i - distance, i) for i in devices if i - distance in devices]
    return lax.ppermute(block, axis, route)


def in_order(parts, dim):
    parts = jnp.moveaxis(parts, 0, dim)
    dims = parts.shape
    return parts.reshape(*dims[:dim], dims[dim] * dims[dim + 1], *dims[dim + 2 :])


def from_everyone(value, axis):
    copies = jnp.broadcast_to(value, (lax.axis_size(axis), *value.shape))
    return lax.all_to_all(copies, axis, split_axis=0, concat_axis=0, tiled=True)


def gathered_copies(value, axis, dim):
    return in_order(from_everyone(value, axis), dim)


def in_blocks(value, dim, peers):
    before, after = (value.shape[:dim], value.shape[dim + 1 :])
    return jnp.moveaxis(value.reshape(*before, peers, -1, *after), dim, 0)


def sum_at_owner(value, axis, dim):
    parts = in_blocks(value, dim, lax.axis_size(axis))
    arrived = lax.all_to_all(parts, axis, split_axis=0, concat_axis=0, tiled=True)
    return arrived.astype(jnp.float32).sum(axis=0)


def in_one_piece(arrays, axis, dim, along):
    columns = [a.reshape(*a.shape[:along], -1) for a in arrays]
    both = jnp.concatenate(columns, axis=along)
    result, at, gathered = (sum_at_owner(both, axis, dim), 0, [])
    for a, column in zip(arrays, columns):
        piece = result[..., at : at + column.shape[along]]
        gathered.append(piece.reshape(*piece.shape[:along], *a.shape[along:]))
        at += column.shape[along]
    return tuple(gathered)


def sent_together(arrays, axis, dim, along):
    ends, at = ([], 0)
    for a in arrays[:-1]:
        at += a.shape[along]
        ends.append(at)
    both = jnp.concatenate(arrays, axis=along)
    return tuple(jnp.split(lax.all_gather(both, axis, axis=dim, tiled=True), ends, axis=along))


def taken_together(value, axis):
    everything = from_everyone(value, axis)
    return jnp.sum(everything.astype(jnp.float32), axis=0)


def rms_scale(values, gain):
    floats = values.astype(jnp.float32)
    return floats * lax.rsqrt(jnp.mean(floats * floats, axis=-1, keepdims=True) + EPS) * gain


def window_attend(query, keys, values, first):
    n_query = query.shape[0]
    n_key = keys.shape[0]
    qh = query.reshape(n_query, BH, HB)
    kh = keys.reshape(n_key, BH, HB)
    vh = values.reshape(n_key, BH, HB)
    scores = jnp.einsum("qhd,khd->hqk", qh, kh, preferred_element_type=jnp.float32) / jnp.sqrt(
        jnp.float32(HB)
    )
    q_pos = first + jnp.arange(n_query, dtype=jnp.int32)
    k_pos = first - (n_key - n_query) + jnp.arange(n_key, dtype=jnp.int32)
    allowed = (
        (k_pos[None, :] <= q_pos[:, None])
        & (k_pos[None, :] > q_pos[:, None] - WIN)
        & (k_pos[None, :] >= 0)
    )
    scores = jnp.where(allowed[None], scores, jnp.float32(-1e30))
    peak = jnp.max(scores, axis=-1, keepdims=True)
    expo = jnp.where(allowed[None], jnp.exp(scores - peak), jnp.float32(0.0))
    total = jnp.sum(expo, axis=-1, keepdims=True)
    mixed = (
        jnp.einsum(
            "hqk,khd->hqd", expo.astype(jnp.bfloat16), vh, preferred_element_type=jnp.float32
        )
        / total
    )
    return jnp.transpose(mixed, (1, 0, 2)).reshape(n_query, BH * HB).astype(jnp.bfloat16)


def local(
    byte_embed,
    patch_start,
    enc_gain,
    enc_qkv,
    enc_out,
    up_proj,
    lat_gain,
    query_proj,
    key_proj,
    value_matrix,
    out_proj,
    down_proj,
):
    nbytes = byte_embed.shape[0]
    width = byte_embed.shape[1]
    n_tp = lax.axis_size("tp")
    n_ctx = lax.axis_size("ctx")
    device = lax.axis_index(("ctx", "tp"))
    group = device // n_tp
    slots = n_tp * nbytes // 4
    normed = rms_scale(byte_embed, enc_gain).astype(jnp.bfloat16)
    qkv = jnp.dot(normed, enc_qkv, preferred_element_type=jnp.float32).astype(jnp.bfloat16)
    query = qkv[:, :width]
    earlier = (qkv[:, width : 2 * width], qkv[:, 2 * width :])
    key_list = [earlier[0]]
    value_list = [earlier[1]]
    for step in range(2):
        earlier = shifted((earlier[0], earlier[1]), ("ctx", "tp"), 1)
        key_list.insert(0, earlier[0])
        value_list.insert(0, earlier[1])
    context = window_attend(
        query,
        jnp.concatenate(key_list, axis=0),
        jnp.concatenate(value_list, axis=0),
        device * nbytes,
    )
    hidden = (
        byte_embed.astype(jnp.float32)
        + jnp.dot(context, enc_out, preferred_element_type=jnp.float32)
    ).astype(jnp.bfloat16)
    local_count = jnp.sum(patch_start)
    all_counts = gathered_copies(local_count[None], ("ctx", "tp"), 0)
    before = jnp.cumsum(all_counts) - all_counts
    offset = before[device] - before[group * n_tp]
    group_counts = jnp.sum(all_counts.reshape(n_ctx, n_tp), axis=1)
    local_slot = jnp.cumsum(patch_start) - 1
    slot = offset + local_slot
    columns = jnp.arange(slots, dtype=jnp.int32)
    onehot = ((slot[:, None] == columns[None, :]) & (local_slot[:, None] >= 0)).astype(jnp.bfloat16)
    part_sum = jnp.dot(onehot.T, hidden, preferred_element_type=jnp.float32)
    part_count = jnp.sum(onehot.astype(jnp.float32), axis=0)
    leading = (local_slot < 0).astype(jnp.bfloat16)
    lead_sum = jnp.dot(leading[None, :], hidden, preferred_element_type=jnp.float32)
    lead_count = jnp.sum(leading.astype(jnp.float32))[None]
    recv_sum, recv_count = shifted((lead_sum, lead_count), ("ctx", "tp"), -1)
    last = offset + local_count - 1
    last_hot = (columns == last).astype(jnp.float32)
    part_sum = part_sum + last_hot[:, None] * recv_sum
    part_count = part_count + last_hot * recv_count
    sums, counts = in_one_piece(
        (part_sum.astype(jnp.bfloat16), part_count.astype(jnp.bfloat16)), "tp", 0, 1
    )
    share = (sums / jnp.maximum(counts, 1.0)[:, None]).astype(jnp.bfloat16)
    pooled = gathered_copies(share, "tp", 0)
    latent_part = jnp.dot(
        pooled,
        lax.all_gather(up_proj, "ctx", axis=0, tiled=True),
        preferred_element_type=jnp.float32,
    ).astype(jnp.bfloat16)
    latent = gathered_copies(latent_part, "tp", 1)
    lnorm = rms_scale(latent, lat_gain).astype(jnp.bfloat16)

    def proj_add(piece):
        return jnp.dot(lnorm, piece, preferred_element_type=jnp.float32)

    pieces = sent_together((query_proj, key_proj, value_matrix), "ctx", 0, 1)
    q_sum, k_sum, v_sum = tuple((proj_add(pieces[i]) for i in range(3)))
    q_local = q_sum.astype(jnp.bfloat16)
    k_local = k_sum.astype(jnp.bfloat16)
    v_local = v_sum.astype(jnp.bfloat16)
    heads_local = q_local.shape[1] // HEAD_SIZE
    kv_local = k_local.shape[1] // HEAD_SIZE
    share_count = heads_local // kv_local
    q_grouped = jnp.transpose(
        q_local.reshape(slots, kv_local, share_count, HEAD_SIZE), (1, 2, 0, 3)
    ).reshape(kv_local, share_count * slots, HEAD_SIZE)
    query_rows = group * slots + jnp.tile(jnp.arange(slots, dtype=jnp.int32), share_count)
    scale = 1.0 / jnp.sqrt(jnp.float32(HEAD_SIZE))
    peak = jnp.full((kv_local, share_count * slots), -1e30, jnp.float32)
    k_piece, v_piece = sent_together((k_local, v_local), "ctx", 0, 1)
    count = k_piece.shape[0]
    k_heads = jnp.transpose(k_piece.reshape(count, kv_local, HEAD_SIZE), (1, 0, 2))
    v_heads = jnp.transpose(v_piece.reshape(count, kv_local, HEAD_SIZE), (1, 0, 2))
    key_rows = jnp.arange(count, dtype=jnp.int32)
    used = key_rows % slots < group_counts[key_rows // slots]
    allowed = used[None, :] & (key_rows[None, :] <= query_rows[:, None])
    scores = (
        jnp.einsum("hqd,hkd->hqk", q_grouped, k_heads, preferred_element_type=jnp.float32) * scale
    )
    scores = jnp.where(allowed[None], scores, jnp.float32(-1e30))
    new_peak = jnp.maximum(peak, jnp.max(scores, axis=-1))
    expo = jnp.where(allowed[None], jnp.exp(scores - new_peak[..., None]), jnp.float32(0.0))
    total = jnp.sum(expo, axis=-1)
    accum = jnp.einsum(
        "hqk,hkd->hqd", expo.astype(jnp.bfloat16), v_heads, preferred_element_type=jnp.float32
    )
    peak, total, accum = (new_peak, total, accum)
    mixed = accum / total[..., None]
    attn = (
        jnp.transpose(mixed.reshape(kv_local, share_count, slots, HEAD_SIZE), (2, 0, 1, 3))
        .reshape(slots, heads_local * HEAD_SIZE)
        .astype(jnp.bfloat16)
    )
    partial_value = jnp.dot(
        attn,
        lax.all_gather(out_proj, "ctx", axis=1, tiled=True),
        preferred_element_type=jnp.float32,
    )
    attn_part = sum_at_owner(partial_value.astype(jnp.bfloat16), "tp", 1)
    latent_out = (latent_part.astype(jnp.float32) + attn_part).astype(jnp.bfloat16)
    down_part = jnp.dot(
        latent_out,
        lax.all_gather(down_proj, "ctx", axis=1, tiled=True),
        preferred_element_type=jnp.float32,
    )
    patch_out = (
        taken_together(down_part.astype(jnp.bfloat16), "tp")
        .astype(jnp.float32)
        .astype(jnp.bfloat16)
    )
    trailing = lax.dynamic_slice_in_dim(patch_out, last, 1, 0)
    carried = shifted(trailing, ("ctx", "tp"), 1)
    spread = jnp.dot(onehot, patch_out, preferred_element_type=jnp.float32) + leading.astype(
        jnp.float32
    )[:, None] * carried.astype(jnp.float32)
    return (hidden.astype(jnp.float32) + spread).astype(jnp.bfloat16)


def solution(mesh):
    placed = (
        P(("dp", "ctx", "tp"), None),
        P(("dp", "ctx", "tp")),
        P(),
        P(),
        P(),
        P("ctx", "tp"),
        P(),
        P("ctx", "tp"),
        P("ctx", "tp"),
        P("ctx", "tp"),
        P("tp", "ctx"),
        P("tp", "ctx"),
    )
    return jax.shard_map(
        local, mesh=mesh, in_specs=placed, out_specs=P(("dp", "ctx", "tp"), None), check_vma=False
    )
```

profile of v0, /device:TPU:64, one launch (start us, length us, event | category | flops | bytes accessed | tf_op | source)
XLA Modules:
  0.0 502.0 jit_solution(70620909785672022)
XLA Ops:
  6.5 0.7 all-gather.6.cloned.1.call-update
  7.3 1.8 pad_maximum_fusion.3
  9.1 1.4 reduce_sum.106
  10.5 1.2 broadcast_in_dim.40
  11.8 13.8 %all-to-all-start = ((s32[64,1,1]{2,1,0:T(1,128)}), s32[64,1,1]{2,1,0:T(1,128)S(1)}, u32[]{:S(2)}, u32[]{:S(2)}) async-start(s32[64,1,1]{2,1,0:T(1,128)} %broadcast_in_dim.40), calls=%async_computation | async-start | bytes 65536 | tf_op jit(solution)/shard_map/all_to_all | solution.py:27
  25.6 1.2 fusion.36
  26.8 4.9 convolution_convert_fusion.1
  31.7 0.9 fusion.72
  32.6 3.4 collective-permute-start
  36.0 3.4 collective-permute-start.2
  40.0 0.6 convert_reduce_fusion.3
  40.6 7.6 %collective-permute-start.5 = (f32[1]{0:T(128)}, f32[1]{0:T(128)}, u32[]{:S(2)}, u32[]{:S(2)}) collective-permute-start(f32[1]{0:T(128)} %bitcast.15), channel_id=1, source_target_pairs={{4,0},{8,4},{12,8},{16,12},{20,16},{24,20},{28,24},{32,28},{36,32}... | collective-permute-start | bytes 20 | tf_op jit(solution)/shard_map/ppermute | solution.py:16
  48.5 1.0 copy.45
  49.8 1.2 reduce.9
  51.0 0.7 fusion.74
  53.0 2.2 collective-permute-done
  55.2 1.9 collective-permute-start.1
  57.2 22.2 %collective-permute-done.2 = bf16[256,1024]{1,0:T(8,128)(2,1)} collective-permute-done((bf16[256,1024]{1,0:T(8,128)(2,1)S(1)}, bf16[256,1024]{1,0:T(8,128)(2,1)}, u32[]{:S(2)}, u32[]{:S(2)}) %collective-permute-start.2) | collective-permute-done | bytes 524320 | tf_op jit(solution)/shard_map/ppermute | solution.py:16
  79.4 1.9 collective-permute-start.3
  82.2 0.6 add_convert_fusion.4
  82.8 7.7 %collective-permute-done.1 = bf16[256,1024]{1,0:T(8,128)(2,1)S(1)} collective-permute-done((bf16[256,1024]{1,0:T(8,128)(2,1)}, bf16[256,1024]{1,0:T(8,128)(2,1)S(1)}, u32[]{:S(2)}, u32[]{:S(2)}) %collective-permute-start.1) | collective-permute-done | bytes 524320 | tf_op jit(solution)/shard_map/ppermute | solution.py:16
  90.5 2.5 pad_maximum_fusion
  93.0 2.6 copy.46
  95.6 5.0 collective-permute-done.3
  100.6 2.5 pad_maximum_fusion.1
  103.1 2.6 copy.47
  105.7 8.4 %fusion.75 = (f32[16,256]{1,0:T(8,128)S(1)}, bf16[16,256,768]{2,1,0:T(8,128)(2,1)}) fusion(pred[256,768]{1,0:T(8,128)(4,1)S(1)} %and_and_fusion, bf16[256,16,64]{0,2,1:T(8,128)(2,1)S(1)} %bitcast.98, bf16[768,16,64]{0,2,1:T(8,128)(2,1)} %bitcast.94), kind=kOutput, calls=%fused_computation.127 | convolution fusion | flops 421528320 | bytes 8601600 | tf_op jit(solution)/shard_map/sub | solution.py:93
  114.1 5.3 %fusion.33 = bf16[256,16,64]{0,2,1:T(8,128)(2,1)S(1)} fusion(bf16[768,16,64]{0,2,1:T(8,128)(2,1)} %bitcast.95, bf16[16,256,768]{2,1,0:T(8,128)(2,1)} %get-tuple-element.30, f32[256,16]{0,1:T(8,128)S(1)} %bitcast.111), kind=kOutput, calls=%fused_computation.41 | convolution fusion | flops 403177472 | bytes 8404992 | tf_op jit(solution)/shard_map/hqk,khd->hqd/dot_general | solution.py:96
  119.4 0.7 fusion.18
  120.3 1.9 collective-permute-start.4
  122.4 3.4 collective-permute-done.4
  125.8 0.4 add_convert_fusion.2
  126.3 10.8 %all_to_all.31 = bf16[4,64,1025]{2,1,0:T(8,128)(2,1)S(1)} all-to-all(bf16[4,64,1025]{2,1,0:T(8,128)(2,1)S(1)} %pad_maximum_fusion.2), channel_id=1, replica_groups=mesh['ctx'=16,'tp'=4,'dp'=4] {'tp'}, dimensions={0} | all-to-all | bytes 1049600 | tf_op jit(solution)/shard_map/all_to_all | solution.py:41
  137.5 10.5 %all_to_all.32 = bf16[4,64,1024]{2,1,0:T(8,128)(2,1)S(1)} all-to-all(bf16[4,64,1024]{2,1,0:T(8,128)(2,1)S(1)} %broadcast_in_dim.42), channel_id=1, replica_groups=mesh['ctx'=16,'tp'=4,'dp'=4] {'tp'}, dimensions={0} | all-to-all | bytes 1048576 | tf_op jit(solution)/shard_map/all_to_all | solution.py:27
  148.0 2.3 convolution_convert_fusion.3
  150.7 25.1 %all_to_all.33 = bf16[4,256,1024]{1,2,0:T(8,128)(2,1)S(1)} all-to-all(bf16[4,256,1024]{1,2,0:T(8,128)(2,1)S(1)} %broadcast_in_dim.43), channel_id=1, replica_groups=mesh['ctx'=16,'tp'=4,'dp'=4] {'tp'}, dimensions={0} | all-to-all | bytes 4194304 | tf_op jit(solution)/shard_map/all_to_all | solution.py:27
  175.7 0.6 multiply_reduce_fusion
  176.3 1.7 fusion.14
  178.0 46.4 %all-gather.8.cloned.1.call-done = bf16[4096,768]{1,0:T(8,128)(2,1)} async-done(((bf16[256,768]{1,0:T(8,128)(2,1)}), bf16[4096,768]{1,0:T(8,128)(2,1)}) %all-gather.8.cloned.1.call-update) | async-done | bytes 6291472 | tf_op jit(solution)/shard_map/all_gather | solution.py:62
  224.5 2.4 convolution_convert_fusion.4
  226.9 2.4 convolution_convert_fusion.5
  229.3 0.7 pad_maximum_fusion.4
  230.1 0.5 all-gather.12.cloned.1.call-update
  230.6 0.5 all-gather.14.cloned.1.call-update
  231.9 0.7 fusion.73
  232.7 4.3 compare_select_fusion.1
  237.0 5.6 %fusion.63 = pred[4096]{0:T(1024)(128)(4,1)S(1)} fusion(pred[4096]{0:T(1024)(128)(4,1)S(1)} %compare_reduce_fusion, pred[4096]{0:T(1024)(128)(4,1)S(1)} %compare_reduce_fusion.1, pred[4096]{0:T(1024)(128)(4,1)S(1)} %compare_reduce_fusion.2, pred[4096]{0:T(1024)(128)(4,1)S(1)} %compare_reduce_fusion.3, pred[4096]{0:T(1024)(128)(4,1)S(1)} %compare_reduce_fusion.4, ...), kind=kLoop, calls=%fused_computation.96 | loop fusion | flops 65536 | bytes 57380 | tf_op jit(solution)/shard_map/lt | solution.py:199
  242.6 3.4 fusion.27
  246.2 60.9 %all-gather.10.cloned.1.call-done = bf16[4096,256]{0,1:T(8,128)(2,1)} async-done(((bf16[256,256]{0,1:T(8,128)(2,1)}), bf16[4096,256]{0,1:T(8,128)(2,1)}) %all-gather.10.cloned.1.call-update) | async-done | bytes 2097168 | tf_op jit(solution)/shard_map/all_gather | solution.py:62
  307.1 6.7 %fusion.2 = (f32[1024]{0:T(1024)S(1)}, f32[1024,4096]{1,0:T(8,128)S(1)}) fusion(s32[1024]{0:T(1024)S(1)} %bitcast.105, pred[4096]{0:T(1024)(128)(4,1)S(1)} %fusion.63, bf16[1024,128]{1,0:T(8,128)(2,1)S(1)} %bitcast.102, bf16[4096,256]{0,1:T(8,128)(2,1)} %all-gather.10.cloned.1.call-done), kind=kOutput, calls=%fused_computation.5 | convolution fusion | flops 1094712320 | bytes 18100224 | tf_op jit(solution)/shard_map/hqd,hkd->hqk/dot_general | solution.py:202
  313.8 7.7 %fusion.70 = f32[1024]{0:T(1024)S(1)} fusion(f32[1024]{0:T(1024)S(1)} %broadcast_maximum_fusion, f32[1024,4096]{1,0:T(8,128)S(1)} %get-tuple-element.32, s32[1024]{0:T(1024)S(1)} %bitcast.106, pred[4096]{0:T(1024)(128)(4,1)S(1)} %fusion.63), kind=kLoop, calls=%fused_computation.123 | loop fusion | flops 29359104 | bytes 16793600 | tf_op jit(solution)/shard_map/reduce_sum | solution.py:207
  321.5 6.0 %fusion.24 = bf16[1024,128]{1,0:T(8,128)(2,1)S(1)} fusion(bf16[4096,256]{0,1:T(8,128)(2,1)S(1)} %copy-done.7, f32[1024]{0:T(1024)S(1)} %fusion.70, f32[1024,4096]{1,0:T(8,128)S(1)} %get-tuple-element.32, f32[1024]{0:T(1024)S(1)} %broadcast_maximum_fusion, s32[1024]{0:T(1024)S(1)} %bitcast.107, pred[4096]{0:T(1024)(128)(4,1)S(1)} %fusion.63), kind=kOutput, calls=%fused_computation.37 | convolution fusion | flops 1103364096 | bytes 18104320 | tf_op jit(solution)/shard_map/hqk,hkd->hqd/dot_general | solution.py:208
  327.6 61.0 %all-gather.12.cloned.1.call-done = bf16[512,4096]{1,0:T(8,128)(2,1)} async-done(((bf16[512,256]{1,0:T(8,128)(2,1)}), bf16[512,4096]{1,0:T(8,128)(2,1)}) %all-gather.12.cloned.1.call-update) | async-done | bytes 4194320 | tf_op jit(solution)/shard_map/all_gather | solution.py:220
  388.6 3.5 convolution_convert_fusion
  392.2 27.1 %all_to_all.34 = bf16[4,256,1024]{2,1,0:T(8,128)(2,1)S(1)} all-to-all(bf16[4,256,1024]{2,1,0:T(8,128)(2,1)S(1)} %bitcast.93), channel_id=1, replica_groups=mesh['ctx'=16,'tp'=4,'dp'=4] {'tp'}, dimensions={0} | all-to-all | bytes 4194304 | tf_op jit(solution)/shard_map/all_to_all | solution.py:41
  419.8 28.2 %all-gather.14.cloned.1.call-done = bf16[1024,1024]{0,1:T(8,128)(2,1)} async-done(((bf16[1024,64]{0,1:T(8,128)(2,1)}), bf16[1024,1024]{0,1:T(8,128)(2,1)}) %all-gather.14.cloned.1.call-update) | async-done | bytes 2097168 | tf_op jit(solution)/shard_map/all_gather | solution.py:227
  448.0 2.3 convolution_convert_fusion.2
  450.4 1.6 broadcast_in_dim.82
  452.0 4.4 all-to-all-start.5
  456.4 25.2 %all-to-all-done.5 = bf16[4,256,1024]{2,1,0:T(8,128)(2,1)} async-done(((bf16[4,256,1024]{2,1,0:T(8,128)(2,1)}), bf16[4,256,1024]{2,1,0:T(8,128)(2,1)}, u32[]{:S(2)}, u32[]{:S(2)}) %all-to-all-start.5) | async-done | bytes 2097184 | tf_op jit(solution)/shard_map/all_to_all | solution.py:27
  481.6 2.0 reduce_sum.115
  483.7 2.5 collective-permute-start.6
  486.2 8.1 %collective-permute-done.6 = bf16[1,1024]{1,0:T(2,128)(2,1)S(1)} collective-permute-done((bf16[1,1024]{1,0:T(2,128)(2,1)S(1)}, bf16[1,1024]{1,0:T(2,128)(2,1)S(1)}, u32[]{:S(2)}, u32[]{:S(2)}) %collective-permute-start.6) | collective-permute-done | bytes 2080 | tf_op jit(solution)/shard_map/ppermute | solution.py:16
  494.3 1.2 add_convert_fusion
  (76 shorter events, 4.2 us)
Async XLA Ops:
  6.5 112.9 %copy-start = (bf16[1024,1024]{1,0:T(8,128)(2,1)S(1)}, bf16[1024,1024]{1,0:T(8,128)(2,1)}, u32[]{:S(2)}) copy-start(bf16[1024,1024]{1,0:T(8,128)(2,1)} %param.16) | copy-start | bytes 6291460
  6.5 141.5 %all-gather.6.cloned.1.call-start = ((), (), s32[]{:S(2)}) async-start(), calls=%async_computation.6 | async-start | bytes 2228224 | tf_op jit(solution)/shard_map/all_gather | solution.py:171
  7.3 217.2 %all-gather.8.cloned.1.call-start = ((), (), s32[]{:S(2)}) async-start(), calls=%async_computation.7 | async-start | bytes 6684672 | tf_op jit(solution)/shard_map/all_gather | solution.py:62
  11.8 37.8 %all-to-all-start = ((s32[64,1,1]{2,1,0:T(1,128)}), s32[64,1,1]{2,1,0:T(1,128)S(1)}, u32[]{:S(2)}, u32[]{:S(2)}) async-start(s32[64,1,1]{2,1,0:T(1,128)} %broadcast_in_dim.40), calls=%async_computation | async-start | bytes 65536 | tf_op jit(solution)/shard_map/all_to_all | solution.py:27
  25.5 281.5 %all-gather.10.cloned.1.call-start = ((), (), s32[]{:S(2)}) async-start(), calls=%async_computation.8 | async-start | bytes 2228224 | tf_op jit(solution)/shard_map/all_gather | solution.py:62
  26.8 12.5 %copy-start.6 = (s32[256]{0:T(256)S(1)}, s32[256]{0:T(256)}, u32[]{:S(2)}) copy-start(s32[256]{0:T(256)} %param.13) | copy-start | bytes 3076
  32.6 22.6 %collective-permute-start = (bf16[256,1024]{1,0:T(8,128)(2,1)}, bf16[256,1024]{1,0:T(8,128)(2,1)}, u32[]{:S(2)}, u32[]{:S(2)}) collective-permute-start(bf16[256,1024]{1,0:T(8,128)(2,1)} %get-tuple-element.8), channel_id=1, source_target_pairs={{0,4},{4,8},{8,12},{12,16},{16,20},{20,24},{24,28},{28,32},{32,36}... | collective-permute-start | bytes 1572872 | tf_op jit(solution)/shard_map/ppermute | solution.py:16
  36.0 43.4 %collective-permute-start.2 = (bf16[256,1024]{1,0:T(8,128)(2,1)S(1)}, bf16[256,1024]{1,0:T(8,128)(2,1)}, u32[]{:S(2)}, u32[]{:S(2)}) collective-permute-start(bf16[256,1024]{1,0:T(8,128)(2,1)S(1)} %get-tuple-element.9), channel_id=1, source_target_pairs={{0,4},{4,8},{8,12},{12,16},{16,20},{20,24},{24,28},{28,32},{32,36}... | collective-permute-start | bytes 1572872 | tf_op jit(solution)/shard_map/ppermute | solution.py:16
  40.6 41.6 %collective-permute-start.5 = (f32[1]{0:T(128)}, f32[1]{0:T(128)}, u32[]{:S(2)}, u32[]{:S(2)}) collective-permute-start(f32[1]{0:T(128)} %bitcast.15), channel_id=1, source_target_pairs={{4,0},{8,4},{12,8},{16,12},{20,16},{24,20},{28,24},{32,28},{36,32}... | collective-permute-start | bytes 20 | tf_op jit(solution)/shard_map/ppermute | solution.py:16
  55.2 35.3 %collective-permute-start.1 = (bf16[256,1024]{1,0:T(8,128)(2,1)}, bf16[256,1024]{1,0:T(8,128)(2,1)S(1)}, u32[]{:S(2)}, u32[]{:S(2)}) collective-permute-start(bf16[256,1024]{1,0:T(8,128)(2,1)} %collective-permute-done), channel_id=1, source_target_pairs={{0,4},{4,8},{8,12},{12,16},{16,20},{20,24},{24,28},{28,32},{32,36}... | collective-permute-start | bytes 1572872 | tf_op jit(solution)/shard_map/ppermute | solution.py:16
  79.4 21.2 %collective-permute-start.3 = (bf16[256,1024]{1,0:T(8,128)(2,1)}, bf16[256,1024]{1,0:T(8,128)(2,1)}, u32[]{:S(2)}, u32[]{:S(2)}) collective-permute-start(bf16[256,1024]{1,0:T(8,128)(2,1)} %collective-permute-done.2), channel_id=1, source_target_pairs={{0,4},{4,8},{8,12},{12,16},{16,20},{20,24},{24,28},{28,32},{32,36}... | collective-permute-start | bytes 1572872 | tf_op jit(solution)/shard_map/ppermute | solution.py:16
  93.0 12.7 %copy-start.4 = (bf16[256,1024]{0,1:T(8,128)(2,1)S(1)}, bf16[256,1024]{0,1:T(8,128)(2,1)}, u32[]{:S(2)}) copy-start(bf16[256,1024]{0,1:T(8,128)(2,1)} %copy.45) | copy-start | bytes 1572868
  114.1 5.3 %copy-start.3 = (bf16[256,1024]{1,0:T(8,128)(2,1)S(1)}, bf16[256,1024]{1,0:T(8,128)(2,1)}, u32[]{:S(2)}) copy-start(bf16[256,1024]{1,0:T(8,128)(2,1)} %param.12) | copy-start | bytes 1572868
  120.3 5.5 %collective-permute-start.4 = (f32[1,1024]{1,0:T(1,128)S(1)}, f32[1,1024]{1,0:T(1,128)S(1)}, u32[]{:S(2)}, u32[]{:S(2)}) collective-permute-start(f32[1,1024]{1,0:T(1,128)S(1)} %fusion.76), channel_id=1, source_target_pairs={{4,0},{8,4},{12,8},{16,12},{20,16},{24,20},{28,24},{32,28},{36,32}... | collective-permute-start | bytes 12296 | tf_op jit(solution)/shard_map/ppermute | solution.py:16
  150.5 25.8 %copy-start.5 = (f32[4096]{0:T(1024)S(1)}, f32[4096]{0:T(1024)}, u32[]{:S(2)}) copy-start(f32[4096]{0:T(1024)} %param.18) | copy-start | bytes 49156
  178.0 64.6 %copy-start.2 = (bf16[256,4096]{0,1:T(8,128)(2,1)S(1)}, bf16[256,4096]{0,1:T(8,128)(2,1)}, u32[]{:S(2)}) copy-start(bf16[256,4096]{0,1:T(8,128)(2,1)} %fusion.14) | copy-start | bytes 6291460
  230.0 158.6 %all-gather.12.cloned.1.call-start = ((), (), s32[]{:S(2)}) async-start(), calls=%async_computation.9 | async-start | bytes 4456448 | tf_op jit(solution)/shard_map/all_gather | solution.py:220
  230.6 217.4 %all-gather.14.cloned.1.call-start = ((), (), s32[]{:S(2)}) async-start(), calls=%async_computation.10 | async-start | bytes 2228224 | tf_op jit(solution)/shard_map/all_gather | solution.py:227
  313.8 7.7 %copy-start.7 = (bf16[4096,256]{0,1:T(8,128)(2,1)S(1)}, bf16[4096,256]{0,1:T(8,128)(2,1)}, u32[]{:S(2)}) copy-start(bf16[4096,256]{0,1:T(8,128)(2,1)} %all-gather.10.cloned.1.call-done) | copy-start | bytes 6291460
  450.4 45.1 %copy-start.1 = (bf16[1024,1024]{1,0:T(8,128)(2,1)S(1)}, bf16[1024,1024]{1,0:T(8,128)(2,1)}, u32[]{:S(2)}) copy-start(bf16[1024,1024]{1,0:T(8,128)(2,1)} %param.16) | copy-start | bytes 6291460
  452.0 29.7 %all-to-all-start.5 = ((bf16[4,256,1024]{2,1,0:T(8,128)(2,1)}), bf16[4,256,1024]{2,1,0:T(8,128)(2,1)}, u32[]{:S(2)}, u32[]{:S(2)}) async-start(bf16[4,256,1024]{2,1,0:T(8,128)(2,1)} %broadcast_in_dim.82), calls=%async_computation.5 | async-start | bytes 4194304 | tf_op jit(solution)/shard_map/all_to_all | solution.py:27
  483.7 10.6 %collective-permute-start.6 = (bf16[1,1024]{1,0:T(2,128)(2,1)S(1)}, bf16[1,1024]{1,0:T(2,128)(2,1)S(1)}, u32[]{:S(2)}, u32[]{:S(2)}) collective-permute-start(bf16[1,1024]{1,0:T(2,128)(2,1)S(1)} %constant_dynamic-slice_fusion), channel_id=1, source_target_pairs={{0,4},{4,8},{8,12},{12,16},{16,20},{20,24},{24,28},{28,32},{32,36}... | collective-permute-start | bytes 6152 | tf_op jit(solution)/shard_map/ppermute | solution.py:16
Sparse Core Ops, SparseCore 0:
  9.8 61.1 all-gather.5
  73.4 151.0 all-gather.7
  230.1 76.9 all-gather.9
  309.3 79.2 all-gather.11
  390.9 57.1 all-gather.13
where the time goes:
time: 503 us; the launch traced here: 502 us
  waiting for transfers between devices  272 us (54%)
  blocking collectives  73.5 us (15%)
  matrix products  50.1 us (10%)
  starting transfers between devices  40.9 us (8%)
  other arithmetic  36.8 us (7%)
  between operations  15.6 us (3%)
  local copies, waits for them, and re-layouts  12.8 us (3%)
    all_gather x2, waiting for transfers between devices, sent_together(): lax.all_gather(both, axis, axis=dim, tiled=True)  107 us
    all_gather x1, waiting for transfers between devices, local(): lax.all_gather(out_proj, 'ctx', axis=1, tiled=True)  61 us
    ppermute x7, waiting for transfers between devices, shifted(): return lax.ppermute(block, axis, route)  48.8 us
    all_to_all x2, blocking collectives, sum_at_owner(): lax.all_to_all(parts, axis, split_axis=0, concat_axis=0, tiled=True)  38 us
    all_to_all x2, blocking collectives, from_everyone(): return lax.all_to_all(copies, axis, split_axis=0, concat_axis=0, tiled=True)  35.6 us
    all_gather x1, waiting for transfers between devices, local(): lax.all_gather(down_proj, 'ctx', axis=1, tiled=True)  28.2 us
    all_to_all x2, waiting for transfers between devices, from_everyone(): return lax.all_to_all(copies, axis, split_axis=0, concat_axis=0, tiled=True)  25.2 us
    ppermute x7, starting transfers between devices, shifted(): return lax.ppermute(block, axis, route)  22.5 us
  transfers between devices with their start and end apart: 14, of which 11 were waited for; matrix products, arithmetic and copies ran while one was open for 17% of the time, Pallas kernels for 0%

commit v1 on v0

--- a/solution.py
+++ b/solution.py
@@ -1,13 +1,30 @@
+import functools
 import jax
 import jax.numpy as jnp
 from jax import lax
 from jax.sharding import PartitionSpec as P
+from jax.lax import all_to_all, axis_size
 
 BH = 16
 HB = 64
 HEAD_SIZE = 128
 WIN = 512
 EPS = 1e-05
+
+
+def return_all_samples_up(local_values, array_axis):
+    return jnp.concatenate(
+        all_to_all(
+            jnp.stack([local_values for _ in range(axis_size("ctx"))], 0),
+            axis_name="ctx",
+            concat_axis=0,
+            split_axis=0,
+        ),
+        axis=array_axis,
+    )
+
+
+_push_column = functools.partial(return_all_samples_up, array_axis=1)
 
 
 def shifted(block, axis, distance):
@@ -215,11 +232,7 @@
         .reshape(slots, heads_local * HEAD_SIZE)
         .astype(jnp.bfloat16)
     )
-    partial_value = jnp.dot(
-        attn,
-        lax.all_gather(out_proj, "ctx", axis=1, tiled=True),
-        preferred_element_type=jnp.float32,
-    )
+    partial_value = jnp.dot(attn, _push_column(out_proj), preferred_element_type=jnp.float32)
     attn_part = sum_at_owner(partial_value.astype(jnp.bfloat16), "tp", 1)
     latent_out = (latent_part.astype(jnp.float32) + attn_part).astype(jnp.bfloat16)
     down_part = jnp.dot(

time: 503 us -> 481 us (0.956)
  waiting for transfers between devices: 272 us -> 236 us
  starting transfers between devices: 40.9 us -> 47.9 us
    all_gather x1 -> x0, waiting for transfers between devices: 61 us -> none  [local(): lax.all_gather(out_proj, 'ctx', axis=1, tiled=True)]
    all_gather x2, waiting for transfers between devices: 107 us -> 153 us  [sent_together(): lax.all_gather(both, axis, axis=dim, tiled=True)]
    all_gather x1, waiting for transfers between devices: 28.2 us -> 7.56 us  [local(): lax.all_gather(down_proj, 'ctx', axis=1, tiled=True)]
    all_to_all x0 -> x1, starting transfers between devices: none -> 7.06 us  [return_all_samples_up(): all_to_all(jnp.stack([local_values for _ in range(axis_size('ctx'))], 0),...]
  transfers between devices with their start and end apart: 14 -> 14, of which waited for: 11 -> 10; matrix products, arithmetic and copies ran while one was open for 17% -> 19% of each run, Pallas kernels for 0% -> 0%
where the time goes in v1:
time: 481 us; the launch traced here: 479 us
  waiting for transfers between devices  236 us (49%)
  blocking collectives  77.5 us (16%)
  matrix products  50.1 us (10%)
  starting transfers between devices  47.9 us (10%)
  other arithmetic  36.9 us (8%)
  between operations  15.6 us (3%)
  local copies, waits for them, and re-layouts  15.4 us (3%)
    all_gather x2, waiting for transfers between devices, sent_together(): lax.all_gather(both, axis, axis=dim, tiled=True)  153 us
    ppermute x7, waiting for transfers between devices, shifted(): return lax.ppermute(block, axis, route)  48.8 us
    all_to_all x2, blocking collectives, sum_at_owner(): lax.all_to_all(parts, axis, split_axis=0, concat_axis=0, tiled=True)  42 us
    all_to_all x2, blocking collectives, from_everyone(): return lax.all_to_all(copies, axis, split_axis=0, concat_axis=0, tiled=True)  35.6 us
    all_to_all x2, waiting for transfers between devices, from_everyone(): return lax.all_to_all(copies, axis, split_axis=0, concat_axis=0, tiled=True)  25.1 us
    ppermute x7, starting transfers between devices, shifted(): return lax.ppermute(block, axis, route)  22.5 us
    all_to_all x2, starting transfers between devices, from_everyone(): return lax.all_to_all(copies, axis, split_axis=0, concat_axis=0, tiled=True)  18.2 us
  transfers between devices with their start and end apart: 14, of which 10 were waited for; matrix products, arithmetic and copies ran while one was open for 19% of the time, Pallas kernels for 0%

profile of v1, /device:TPU:64, one launch (start us, length us, event | category | flops | bytes accessed | tf_op | source)
XLA Modules:
  0.0 479.2 jit_solution(5023694886515261013)
XLA Ops:
  6.5 0.7 all-gather.5.cloned.1.call-update
  7.3 1.8 pad_maximum_fusion.3
  9.1 1.4 reduce_sum.106
  10.5 1.2 broadcast_in_dim.40
  11.8 13.8 %all-to-all-start = ((s32[64,1,1]{2,1,0:T(1,128)}), s32[64,1,1]{2,1,0:T(1,128)S(1)}, u32[]{:S(2)}, u32[]{:S(2)}) async-start(s32[64,1,1]{2,1,0:T(1,128)} %broadcast_in_dim.40), calls=%async_computation | async-start | bytes 65536 | tf_op jit(solution)/shard_map/all_to_all | solution.py:44
  25.6 1.2 fusion.36
  26.8 4.9 %convolution_convert_fusion.1 = bf16[256,3072]{1,0:T(8,128)(2,1)S(1)} fusion(bf16[1024,3072]{1,0:T(8,128)(2,1)} %param.15, bf16[256,1024]{1,0:T(8,128)(2,1)} %param.12, f32[1024]{0:T(1024)} %param.14, f32[256]{0:T(256)S(1)} %add_rsqrt_fusion.1), kind=kOutput, calls=%fused_computation.24 | convolution fusion | flops 1612447744 | bytes 8393728 | tf_op jit(solution)/shard_map/dot_general | solution.py:143
  31.7 0.9 fusion.72
  32.6 3.4 collective-permute-start
  36.0 3.4 collective-permute-start.2
  40.0 0.6 convert_reduce_fusion.3
  40.6 7.6 %collective-permute-start.5 = (f32[1]{0:T(128)}, f32[1]{0:T(128)}, u32[]{:S(2)}, u32[]{:S(2)}) collective-permute-start(f32[1]{0:T(128)} %bitcast.15), channel_id=1, source_target_pairs={{4,0},{8,4},{12,8},{16,12},{20,16},{24,20},{28,24},{32,28},{36,32}... | collective-permute-start | bytes 20 | tf_op jit(solution)/shard_map/ppermute | solution.py:33
  48.5 1.0 copy.48
  49.8 1.2 reduce.9
  51.0 0.7 fusion.74
  53.0 2.2 collective-permute-done
  55.2 1.9 collective-permute-start.1
  57.2 22.2 %collective-permute-done.2 = bf16[256,1024]{1,0:T(8,128)(2,1)} collective-permute-done((bf16[256,1024]{1,0:T(8,128)(2,1)S(1)}, bf16[256,1024]{1,0:T(8,128)(2,1)}, u32[]{:S(2)}, u32[]{:S(2)}) %collective-permute-start.2) | collective-permute-done | bytes 524320 | tf_op jit(solution)/shard_map/ppermute | solution.py:33
  79.4 1.9 collective-permute-start.3
  82.2 0.6 add_convert_fusion.4
  82.8 7.7 %collective-permute-done.1 = bf16[256,1024]{1,0:T(8,128)(2,1)S(1)} collective-permute-done((bf16[256,1024]{1,0:T(8,128)(2,1)}, bf16[256,1024]{1,0:T(8,128)(2,1)S(1)}, u32[]{:S(2)}, u32[]{:S(2)}) %collective-permute-start.1) | collective-permute-done | bytes 524320 | tf_op jit(solution)/shard_map/ppermute | solution.py:33
  90.5 2.5 pad_maximum_fusion
  93.0 2.6 copy.49
  95.6 5.0 %collective-permute-done.3 = bf16[256,1024]{1,0:T(8,128)(2,1)} collective-permute-done((bf16[256,1024]{1,0:T(8,128)(2,1)}, bf16[256,1024]{1,0:T(8,128)(2,1)}, u32[]{:S(2)}, u32[]{:S(2)}) %collective-permute-start.3) | collective-permute-done | bytes 524320 | tf_op jit(solution)/shard_map/ppermute | solution.py:33
  100.6 2.5 pad_maximum_fusion.1
  103.1 2.6 copy.50
  105.7 8.4 %fusion.75 = (f32[16,256]{1,0:T(8,128)S(1)}, bf16[16,256,768]{2,1,0:T(8,128)(2,1)}) fusion(pred[256,768]{1,0:T(8,128)(4,1)S(1)} %and_and_fusion, bf16[256,16,64]{0,2,1:T(8,128)(2,1)S(1)} %bitcast.101, bf16[768,16,64]{0,2,1:T(8,128)(2,1)} %bitcast.97), kind=kOutput, calls=%fused_computation.127 | convolution fusion | flops 421528320 | bytes 8601600 | tf_op jit(solution)/shard_map/sub | solution.py:110
  114.1 5.3 %fusion.33 = bf16[256,16,64]{0,2,1:T(8,128)(2,1)S(1)} fusion(bf16[768,16,64]{0,2,1:T(8,128)(2,1)} %bitcast.98, bf16[16,256,768]{2,1,0:T(8,128)(2,1)} %get-tuple-element.30, f32[256,16]{0,1:T(8,128)S(1)} %bitcast.114), kind=kOutput, calls=%fused_computation.41 | convolution fusion | flops 403177472 | bytes 8404992 | tf_op jit(solution)/shard_map/hqk,khd->hqd/dot_general | solution.py:113
  119.4 0.7 fusion.18
  120.3 1.9 collective-permute-start.4
  122.4 3.4 collective-permute-done.4
  125.8 0.4 add_convert_fusion.2
  126.3 10.8 %all_to_all.36 = bf16[4,64,1025]{2,1,0:T(8,128)(2,1)S(1)} all-to-all(bf16[4,64,1025]{2,1,0:T(8,128)(2,1)S(1)} %pad_maximum_fusion.2), channel_id=1, replica_groups=mesh['ctx'=16,'tp'=4,'dp'=4] {'tp'}, dimensions={0} | all-to-all | bytes 1049600 | tf_op jit(solution)/shard_map/all_to_all | solution.py:58
  137.5 10.5 %all_to_all.37 = bf16[4,64,1024]{2,1,0:T(8,128)(2,1)S(1)} all-to-all(bf16[4,64,1024]{2,1,0:T(8,128)(2,1)S(1)} %broadcast_in_dim.42), channel_id=1, replica_groups=mesh['ctx'=16,'tp'=4,'dp'=4] {'tp'}, dimensions={0} | all-to-all | bytes 1048576 | tf_op jit(solution)/shard_map/all_to_all | solution.py:44
  148.0 2.3 convolution_convert_fusion.3
  150.7 25.1 %all_to_all.38 = bf16[4,256,1024]{1,2,0:T(8,128)(2,1)S(1)} all-to-all(bf16[4,256,1024]{1,2,0:T(8,128)(2,1)S(1)} %broadcast_in_dim.43), channel_id=1, replica_groups=mesh['ctx'=16,'tp'=4,'dp'=4] {'tp'}, dimensions={0} | all-to-all | bytes 4194304 | tf_op jit(solution)/shard_map/all_to_all | solution.py:44
  175.7 0.6 multiply_reduce_fusion
  176.3 1.7 fusion.14
  178.0 46.5 %all-gather.7.cloned.1.call-done = bf16[4096,768]{1,0:T(8,128)(2,1)} async-done(((bf16[256,768]{1,0:T(8,128)(2,1)}), bf16[4096,768]{1,0:T(8,128)(2,1)}) %all-gather.7.cloned.1.call-update) | async-done | bytes 6291472 | tf_op jit(solution)/shard_map/all_gather | solution.py:79
  224.5 2.4 convolution_convert_fusion.4
  226.9 2.4 convolution_convert_fusion.5
  229.3 0.7 pad_maximum_fusion.4
  230.2 2.5 stack.2
  232.7 7.1 %all-to-all-start.4 = ((bf16[16,512,256]{1,2,0:T(8,128)(2,1)}), bf16[16,512,256]{1,2,0:T(8,128)(2,1)}, u32[]{:S(2)}, u32[]{:S(2)}) async-start(bf16[16,512,256]{1,2,0:T(8,128)(2,1)} %stack.2), calls=%async_computation.4 | async-start | bytes 8388608 | tf_op jit(solution)/shard_map/all_to_all | solution.py:17
  239.8 0.5 all-gather.11.cloned.1.call-update
  241.1 0.7 fusion.73
  241.8 4.5 compare_select_fusion.1
  246.3 5.6 %fusion.63 = pred[4096]{0:T(1024)(128)(4,1)S(1)} fusion(pred[4096]{0:T(1024)(128)(4,1)S(1)} %compare_reduce_fusion, pred[4096]{0:T(1024)(128)(4,1)S(1)} %compare_reduce_fusion.1, pred[4096]{0:T(1024)(128)(4,1)S(1)} %compare_reduce_fusion.2, pred[4096]{0:T(1024)(128)(4,1)S(1)} %compare_reduce_fusion.3, pred[4096]{0:T(1024)(128)(4,1)S(1)} %compare_reduce_fusion.4, ...), kind=kLoop, calls=%fused_computation.96 | loop fusion | flops 65536 | bytes 57380 | tf_op jit(solution)/shard_map/lt | solution.py:216
  251.8 3.4 fusion.27
  255.4 106.6 %all-gather.9.cloned.1.call-done = bf16[4096,256]{0,1:T(8,128)(2,1)} async-done(((bf16[256,256]{0,1:T(8,128)(2,1)}), bf16[4096,256]{0,1:T(8,128)(2,1)}) %all-gather.9.cloned.1.call-update) | async-done | bytes 2097168 | tf_op jit(solution)/shard_map/all_gather | solution.py:79
  362.0 6.7 %fusion.2 = (f32[1024]{0:T(1024)S(1)}, f32[1024,4096]{1,0:T(8,128)S(1)}) fusion(s32[1024]{0:T(1024)S(1)} %bitcast.108, pred[4096]{0:T(1024)(128)(4,1)S(1)} %fusion.63, bf16[1024,128]{1,0:T(8,128)(2,1)S(1)} %bitcast.105, bf16[4096,256]{0,1:T(8,128)(2,1)} %all-gather.9.cloned.1.call-done), kind=kOutput, calls=%fused_computation.5 | convolution fusion | flops 1094712320 | bytes 18100224 | tf_op jit(solution)/shard_map/hqd,hkd->hqk/dot_general | solution.py:219
  368.7 7.7 %fusion.70 = f32[1024]{0:T(1024)S(1)} fusion(f32[1024]{0:T(1024)S(1)} %broadcast_maximum_fusion, f32[1024,4096]{1,0:T(8,128)S(1)} %get-tuple-element.32, s32[1024]{0:T(1024)S(1)} %bitcast.109, pred[4096]{0:T(1024)(128)(4,1)S(1)} %fusion.63), kind=kLoop, calls=%fused_computation.123 | loop fusion | flops 29359104 | bytes 16793600 | tf_op jit(solution)/shard_map/reduce_sum | solution.py:224
  376.4 6.0 %fusion.24 = bf16[1024,128]{1,0:T(8,128)(2,1)S(1)} fusion(bf16[4096,256]{0,1:T(8,128)(2,1)S(1)} %copy-done.8, f32[1024]{0:T(1024)S(1)} %fusion.70, f32[1024,4096]{1,0:T(8,128)S(1)} %get-tuple-element.32, f32[1024]{0:T(1024)S(1)} %broadcast_maximum_fusion, s32[1024]{0:T(1024)S(1)} %bitcast.110, pred[4096]{0:T(1024)(128)(4,1)S(1)} %fusion.63), kind=kOutput, calls=%fused_computation.37 | convolution fusion | flops 1103364096 | bytes 18104320 | tf_op jit(solution)/shard_map/hqk,hkd->hqd/dot_general | solution.py:225
  382.6 3.5 convolution_convert_fusion
  386.3 31.2 %all_to_all.39 = bf16[4,256,1024]{2,1,0:T(8,128)(2,1)S(1)} all-to-all(bf16[4,256,1024]{2,1,0:T(8,128)(2,1)S(1)} %bitcast.96), channel_id=1, replica_groups=mesh['ctx'=16,'tp'=4,'dp'=4] {'tp'}, dimensions={0} | all-to-all | bytes 4194304 | tf_op jit(solution)/shard_map/all_to_all | solution.py:58
  417.8 7.6 %all-gather.11.cloned.1.call-done = bf16[1024,1024]{0,1:T(8,128)(2,1)} async-done(((bf16[1024,64]{0,1:T(8,128)(2,1)}), bf16[1024,1024]{0,1:T(8,128)(2,1)}) %all-gather.11.cloned.1.call-update) | async-done | bytes 2097168 | tf_op jit(solution)/shard_map/all_gather | solution.py:240
  425.4 2.3 convolution_convert_fusion.2
  427.7 1.6 broadcast_in_dim.82
  429.3 4.4 all-to-all-start.6
  433.8 25.1 %all-to-all-done.6 = bf16[4,256,1024]{2,1,0:T(8,128)(2,1)} async-done(((bf16[4,256,1024]{2,1,0:T(8,128)(2,1)}), bf16[4,256,1024]{2,1,0:T(8,128)(2,1)}, u32[]{:S(2)}, u32[]{:S(2)}) %all-to-all-start.6) | async-done | bytes 2097184 | tf_op jit(solution)/shard_map/all_to_all | solution.py:44
  458.9 2.0 reduce_sum.115
  460.9 2.5 collective-permute-start.6
  463.4 8.1 %collective-permute-done.6 = bf16[1,1024]{1,0:T(2,128)(2,1)S(1)} collective-permute-done((bf16[1,1024]{1,0:T(2,128)(2,1)S(1)}, bf16[1,1024]{1,0:T(2,128)(2,1)S(1)}, u32[]{:S(2)}, u32[]{:S(2)}) %collective-permute-start.6) | collective-permute-done | bytes 2080 | tf_op jit(solution)/shard_map/ppermute | solution.py:33
  471.6 1.2 add_convert_fusion
  (79 shorter events, 4.4 us)
Async XLA Ops:
  6.5 112.9 %copy-start = (bf16[1024,1024]{1,0:T(8,128)(2,1)S(1)}, bf16[1024,1024]{1,0:T(8,128)(2,1)}, u32[]{:S(2)}) copy-start(bf16[1024,1024]{1,0:T(8,128)(2,1)} %param.16) | copy-start | bytes 6291460
  6.5 141.5 %all-gather.5.cloned.1.call-start = ((), (), s32[]{:S(2)}) async-start(), calls=%async_computation.7 | async-start | bytes 2228224 | tf_op jit(solution)/shard_map/all_gather | solution.py:188
  7.3 217.2 %all-gather.7.cloned.1.call-start = ((), (), s32[]{:S(2)}) async-start(), calls=%async_computation.8 | async-start | bytes 6684672 | tf_op jit(solution)/shard_map/all_gather | solution.py:79
  11.8 37.8 %all-to-all-start = ((s32[64,1,1]{2,1,0:T(1,128)}), s32[64,1,1]{2,1,0:T(1,128)S(1)}, u32[]{:S(2)}, u32[]{:S(2)}) async-start(s32[64,1,1]{2,1,0:T(1,128)} %broadcast_in_dim.40), calls=%async_computation | async-start | bytes 65536 | tf_op jit(solution)/shard_map/all_to_all | solution.py:44
  25.5 336.4 %all-gather.9.cloned.1.call-start = ((), (), s32[]{:S(2)}) async-start(), calls=%async_computation.9 | async-start | bytes 2228224 | tf_op jit(solution)/shard_map/all_gather | solution.py:79
  26.8 12.5 %copy-start.7 = (s32[256]{0:T(256)S(1)}, s32[256]{0:T(256)}, u32[]{:S(2)}) copy-start(s32[256]{0:T(256)} %param.13) | copy-start | bytes 3076
  32.6 22.6 %collective-permute-start = (bf16[256,1024]{1,0:T(8,128)(2,1)}, bf16[256,1024]{1,0:T(8,128)(2,1)}, u32[]{:S(2)}, u32[]{:S(2)}) collective-permute-start(bf16[256,1024]{1,0:T(8,128)(2,1)} %get-tuple-element.8), channel_id=1, source_target_pairs={{0,4},{4,8},{8,12},{12,16},{16,20},{20,24},{24,28},{28,32},{32,36}... | collective-permute-start | bytes 1572872 | tf_op jit(solution)/shard_map/ppermute | solution.py:33
  36.0 43.4 %collective-permute-start.2 = (bf16[256,1024]{1,0:T(8,128)(2,1)S(1)}, bf16[256,1024]{1,0:T(8,128)(2,1)}, u32[]{:S(2)}, u32[]{:S(2)}) collective-permute-start(bf16[256,1024]{1,0:T(8,128)(2,1)S(1)} %get-tuple-element.9), channel_id=1, source_target_pairs={{0,4},{4,8},{8,12},{12,16},{16,20},{20,24},{24,28},{28,32},{32,36}... | collective-permute-start | bytes 1572872 | tf_op jit(solution)/shard_map/ppermute | solution.py:33
  40.6 41.6 %collective-permute-start.5 = (f32[1]{0:T(128)}, f32[1]{0:T(128)}, u32[]{:S(2)}, u32[]{:S(2)}) collective-permute-start(f32[1]{0:T(128)} %bitcast.15), channel_id=1, source_target_pairs={{4,0},{8,4},{12,8},{16,12},{20,16},{24,20},{28,24},{32,28},{36,32}... | collective-permute-start | bytes 20 | tf_op jit(solution)/shard_map/ppermute | solution.py:33
  55.2 35.3 %collective-permute-start.1 = (bf16[256,1024]{1,0:T(8,128)(2,1)}, bf16[256,1024]{1,0:T(8,128)(2,1)S(1)}, u32[]{:S(2)}, u32[]{:S(2)}) collective-permute-start(bf16[256,1024]{1,0:T(8,128)(2,1)} %collective-permute-done), channel_id=1, source_target_pairs={{0,4},{4,8},{8,12},{12,16},{16,20},{20,24},{24,28},{28,32},{32,36}... | collective-permute-start | bytes 1572872 | tf_op jit(solution)/shard_map/ppermute | solution.py:33
  79.4 21.2 %collective-permute-start.3 = (bf16[256,1024]{1,0:T(8,128)(2,1)}, bf16[256,1024]{1,0:T(8,128)(2,1)}, u32[]{:S(2)}, u32[]{:S(2)}) collective-permute-start(bf16[256,1024]{1,0:T(8,128)(2,1)} %collective-permute-done.2), channel_id=1, source_target_pairs={{0,4},{4,8},{8,12},{12,16},{16,20},{20,24},{24,28},{28,32},{32,36}... | collective-permute-start | bytes 1572872 | tf_op jit(solution)/shard_map/ppermute | solution.py:33
  93.0 12.7 %copy-start.4 = (bf16[256,1024]{0,1:T(8,128)(2,1)S(1)}, bf16[256,1024]{0,1:T(8,128)(2,1)}, u32[]{:S(2)}) copy-start(bf16[256,1024]{0,1:T(8,128)(2,1)} %copy.48) | copy-start | bytes 1572868
  114.1 5.3 %copy-start.3 = (bf16[256,1024]{1,0:T(8,128)(2,1)S(1)}, bf16[256,1024]{1,0:T(8,128)(2,1)}, u32[]{:S(2)}) copy-start(bf16[256,1024]{1,0:T(8,128)(2,1)} %param.12) | copy-start | bytes 1572868
  120.3 5.5 %collective-permute-start.4 = (f32[1,1024]{1,0:T(1,128)S(1)}, f32[1,1024]{1,0:T(1,128)S(1)}, u32[]{:S(2)}, u32[]{:S(2)}) collective-permute-start(f32[1,1024]{1,0:T(1,128)S(1)} %fusion.76), channel_id=1, source_target_pairs={{4,0},{8,4},{12,8},{16,12},{20,16},{24,20},{28,24},{32,28},{36,32}... | collective-permute-start | bytes 12296 | tf_op jit(solution)/shard_map/ppermute | solution.py:33
  150.5 25.8 %copy-start.6 = (f32[4096]{0:T(1024)S(1)}, f32[4096]{0:T(1024)}, u32[]{:S(2)}) copy-start(f32[4096]{0:T(1024)} %param.18) | copy-start | bytes 49156
  178.0 52.0 %copy-start.5 = (bf16[512,256]{1,0:T(8,128)(2,1)S(1)}, bf16[512,256]{1,0:T(8,128)(2,1)}, u32[]{:S(2)}) copy-start(bf16[512,256]{1,0:T(8,128)(2,1)} %param.22) | copy-start | bytes 786436
  232.7 19.2 %copy-start.2 = (bf16[256,4096]{0,1:T(8,128)(2,1)S(1)}, bf16[256,4096]{0,1:T(8,128)(2,1)}, u32[]{:S(2)}) copy-start(bf16[256,4096]{0,1:T(8,128)(2,1)} %fusion.14) | copy-start | bytes 6291460
  232.7 149.9 %all-to-all-start.4 = ((bf16[16,512,256]{1,2,0:T(8,128)(2,1)}), bf16[16,512,256]{1,2,0:T(8,128)(2,1)}, u32[]{:S(2)}, u32[]{:S(2)}) async-start(bf16[16,512,256]{1,2,0:T(8,128)(2,1)} %stack.2), calls=%async_computation.4 | async-start | bytes 8388608 | tf_op jit(solution)/shard_map/all_to_all | solution.py:17
  239.7 185.7 %all-gather.11.cloned.1.call-start = ((), (), s32[]{:S(2)}) async-start(), calls=%async_computation.10 | async-start | bytes 2228224 | tf_op jit(solution)/shard_map/all_gather | solution.py:240
  368.7 7.7 %copy-start.8 = (bf16[4096,256]{0,1:T(8,128)(2,1)S(1)}, bf16[4096,256]{0,1:T(8,128)(2,1)}, u32[]{:S(2)}) copy-start(bf16[4096,256]{0,1:T(8,128)(2,1)} %all-gather.9.cloned.1.call-done) | copy-start | bytes 6291460
  427.7 45.0 %copy-start.1 = (bf16[1024,1024]{1,0:T(8,128)(2,1)S(1)}, bf16[1024,1024]{1,0:T(8,128)(2,1)}, u32[]{:S(2)}) copy-start(bf16[1024,1024]{1,0:T(8,128)(2,1)} %param.16) | copy-start | bytes 6291460
  429.3 29.6 %all-to-all-start.6 = ((bf16[4,256,1024]{2,1,0:T(8,128)(2,1)}), bf16[4,256,1024]{2,1,0:T(8,128)(2,1)}, u32[]{:S(2)}, u32[]{:S(2)}) async-start(bf16[4,256,1024]{2,1,0:T(8,128)(2,1)} %broadcast_in_dim.82), calls=%async_computation.6 | async-start | bytes 4194304 | tf_op jit(solution)/shard_map/all_to_all | solution.py:44
  460.9 10.6 %collective-permute-start.6 = (bf16[1,1024]{1,0:T(2,128)(2,1)S(1)}, bf16[1,1024]{1,0:T(2,128)(2,1)S(1)}, u32[]{:S(2)}, u32[]{:S(2)}) collective-permute-start(bf16[1,1024]{1,0:T(2,128)(2,1)S(1)} %constant_dynamic-slice_fusion), channel_id=1, source_target_pairs={{0,4},{4,8},{8,12},{12,16},{16,20},{20,24},{24,28},{28,32},{32,36}... | collective-permute-start | bytes 6152 | tf_op jit(solution)/shard_map/ppermute | solution.py:33
Sparse Core Ops, SparseCore 0:
  9.8 61.1 all-gather.4
  73.4 151.0 all-gather.6
  230.1 131.8 all-gather.8
  364.3 61.0 all-gather.10
